TPU v7x, 32 devices: a whole 2x2x4 slice. The times are simulated.
32 devices in a mesh: seq: 16 (over z, y, x), head: 2 (over core).
Axes of the slice: x: 2, y: 2, z: 4, core: 2. Of those that a mesh axis runs over, the one named last changes fastest.
Arguments:
- hidden: bfloat16 [8192, 8192], P('seq', 'head'), may hold values from -6 to 6
- key_weight: bfloat16 [8192, 1024], P('head'), may hold values from -0.0625 to 0.0625
- value_weight: bfloat16 [8192, 1024], P('head'), may hold values from -0.0625 to 0.0625
- key_bias: float32 [1024], P('head'), may hold values from -5 to 5
- value_bias: float32 [1024], P('head'), may hold values from -5 to 5
- request_tokens: int32 [16], replicated, may hold values from 1 to 1024, 8192 in all
- request_context: int32 [16], replicated, may hold values from 0 to 4095
- page_owner: int32 [1024], replicated, may hold values from 0 to 15, as said below
- page_slot: int32 [1024], replicated, may hold values from 0 to 78
- key_cache: bfloat16 [1264, 8, 1024], P('seq', None, 'head'), may hold values from -1 to 1
- value_cache: bfloat16 [1264, 8, 1024], P('seq', None, 'head'), may hold values from -1 to 1
- stored_key_scales: bfloat16 [1264, 8], P('seq', 'head'), may hold values from 0.5 to 8
- value_scales: bfloat16 [1264, 8], P('seq', 'head'), may hold values from 0.5 to 8
Outputs:
- new_key_cache: bfloat16 [1264, 8, 1024], P('seq', None, 'head')
- new_value_cache: bfloat16 [1264, 8, 1024], P('seq', None, 'head')
- new_key_scales: bfloat16 [1264, 8], P('seq', 'head')
- new_value_scales: bfloat16 [1264, 8], P('seq', 'head')
Inputs may be any that keep to these rules, and one draw needn't show every extreme that they name: No two pages name the same (page_owner, page_slot) pair. Each index of seq owns at most 79 pages of the block, and one owns exactly 79 in every draw. The 64 pages of one index of seq (pages i * 64 to (i + 1) * 64 - 1) go at most 5 to one owner, and some index sends exactly 5 to one owner in every draw.
All inputs are finite; a program needn't handle non-finite values.
Results may differ from a plain program's by a relative error of at most 0.0065.
Values may be sent and summed in bfloat16 or wider, within the bound.
A program may use at most 128 MiB of HBM per device.

v0:
```python
import functools

import jax
import jax.numpy as jnp
from jax import lax
from jax.experimental import pallas as pl
from jax.experimental.pallas import tpu as pltpu
from jax.sharding import PartitionSpec as P

rope_base = 1000000.0
eps = 1e-06
KS = 4
MESH = pl.DeviceIdType.MESH


def body(
    n, cap, heads, hd, page,
    own_in, slot_in, freq_in, kb_in, vb_in, oks_in, ovs_in, rt_in, rc_in,
    h_hbm, kw_hbm, vw_hbm, kc_hbm, vc_hbm,
    kc_out, vc_out, ks_out, vs_out,
    h_v, w_v, p_v, u_v, part_s, part_r, own_v, bias_v, send_v, recv_v, cache_v, scale_v,
    cos_v, sin_v, sr_v,
    own_ref, slot_ref, freq_ref, kb_ref, vb_ref, oks_ref, ovs_ref, rt_ref, rc_ref,
    h_sem, w_sem, c_sem, o_sem, ps_sem, pr_sem, s_sem, r_sem, l_sem, i_sem,
):
    toks, kd = h_v.shape[1:]
    depth = KS * kd
    wide = 2 * hd
    half_cols = heads * hd
    per = half_cols // wide
    chunks = 2 * per

    me = lax.axis_index("seq")
    side = lax.axis_index("head")
    other = 1 - side
    slots = cache_v.shape[1]

    def w_copy(c, o, s):
        src = vw_hbm if c < per else kw_hbm
        col = (other if o == 0 else side) * half_cols + (c % per) * wide
        col = pl.multiple_of(col, wide)
        return pltpu.make_async_copy(
            src.at[pl.ds(s * kd, kd), pl.ds(col, wide)],
            w_v.at[c, o, pl.ds(s * kd, kd)],
            w_sem.at[c, o, s],
        )

    def h_copy(s):
        return pltpu.make_async_copy(
            h_hbm.at[:, pl.ds(s * kd, kd)], h_v.at[s], h_sem.at[s]
        )

    def cache_in(c):
        src = vc_hbm if c < per else kc_hbm
        return pltpu.make_async_copy(
            src.at[:, :, pl.ds((c % per) * wide, wide)], cache_v.at[c], c_sem.at[c]
        )

    def cache_out(c):
        dst = vc_out if c < per else kc_out
        return pltpu.make_async_copy(
            cache_v.at[c], dst.at[:, :, pl.ds((c % per) * wide, wide)], o_sem.at[c]
        )

    pairs = (
        (own_in, own_ref), (slot_in, slot_ref), (freq_in, freq_ref), (kb_in, kb_ref),
        (vb_in, vb_ref), (oks_in, oks_ref), (ovs_in, ovs_ref), (rt_in, rt_ref), (rc_in, rc_ref),
    )
    small = [
        pltpu.make_async_copy(src, dst, i_sem.at[i]) for i, (src, dst) in enumerate(pairs)
    ]
    for copy in small:
        copy.start()
    for s in range(KS):
        h_copy(s).start()
        w_copy(0, 0, s).start()
    for s in range(KS):
        w_copy(0, 1, s).start()

    barrier = pltpu.get_barrier_semaphore()
    pl.semaphore_signal(barrier, inc=1, device_id={"head": other}, device_id_type=MESH)

    def greet(k, carry):
        pl.semaphore_signal(
            barrier, inc=1, device_id={"seq": lax.rem(me + k, n)}, device_id_type=MESH
        )
        return carry

    lax.fori_loop(1, n, greet, 0)
    for copy in small:
        copy.wait()

    for c in range(chunks):
        src = vb_ref if c < per else kb_ref
        bias_v[c] = src[:, pl.ds((c % per) * wide, wide)]
    total_pages = own_ref.shape[1]
    here = total_pages // n
    f32 = jnp.float32
    owner = own_ref[...]
    gid = lax.broadcasted_iota(jnp.int32, (1, total_pages), 1)
    within = gid % here
    match = lax.broadcasted_iota(jnp.int32, (n, total_pages), 0) == owner
    count = jnp.where(match, 1.0, 0.0)
    shift = 1
    while shift < here:
        count = count + jnp.where(within >= shift, pltpu.roll(count, shift, 1), 0.0)
        shift *= 2
    rank = jnp.sum(jnp.where(match, count, 0.0), axis=0, keepdims=True) - 1.0
    place = ((owner - me + n) % n * cap).astype(f32) + rank
    place = pltpu.roll(
        jnp.broadcast_to(place, (8, total_pages)), (total_pages - me * here) % total_pages, 1
    )[:, :here]
    expand = (
        lax.broadcasted_iota(jnp.int32, (here, toks), 0)
        == lax.broadcasted_iota(jnp.int32, (here, toks), 1) // page
    )
    place = jnp.dot(
        place.astype(jnp.bfloat16),
        jnp.where(expand, 1.0, 0.0).astype(jnp.bfloat16),
        preferred_element_type=f32,
    )[:1]
    token = lax.broadcasted_iota(jnp.int32, (1, toks), 1)
    dk = place * page + (token % page).astype(f32)
    rows = lax.broadcasted_iota(jnp.int32, p_v.shape, 0).astype(f32)
    p_v[...] = jnp.where(rows == dk, 1.0, 0.0).astype(jnp.bfloat16)

    def unpack_table():
        slot = jnp.where(owner == me, slot_ref[...], -1)
        lane = (((me - gid // here + n) % n) * cap).astype(f32) + rank + 1.0
        want = lax.broadcasted_iota(jnp.int32, (u_v.shape[0], 1), 0)
        src = jnp.sum(jnp.where(want // page == slot, lane, 0.0), axis=1, keepdims=True) - 1.0
        sr_v[...] = jnp.where(src >= 0.0, src * page + (want % page).astype(f32), -1.0)
        lanes = lax.broadcasted_iota(jnp.int32, u_v.shape, 1).astype(f32)
        u_v[...] = jnp.where(lanes == sr_v[...], 1.0, 0.0).astype(jnp.bfloat16)

    def rope_table():
        token_ids = me * toks + lax.broadcasted_iota(jnp.int32, cos_v.shape, 0)
        offset = jnp.zeros_like(token_ids)
        start = jnp.int32(0)
        for r in range(rt_ref.shape[0]):
            offset = jnp.where(token_ids >= start, rc_ref[r] - start, offset)
            start = start + rt_ref[r]
        angle = (offset + token_ids).astype(f32) * freq_ref[...]
        cos_v[...] = jnp.cos(angle)
        sine = jnp.sin(angle)
        front = lax.broadcasted_iota(jnp.int32, cos_v.shape, 1) < hd // 2
        sin_v[...] = jnp.where(front, -sine, sine)

    cos_v[...] = jnp.ones_like(cos_v)
    sin_v[...] = jnp.zeros_like(sin_v)
    scale_v[...] = jnp.zeros_like(scale_v)

    def partial(c, o, out, first):
        def step(s, carry):
            @pl.when(jnp.logical_and(c == 0, first))
            def _():
                pltpu.make_async_copy(h_v.at[s], h_v.at[s], h_sem.at[s]).wait()

            w_slice = w_v.at[c, o, pl.ds(pl.multiple_of(s * kd, kd), kd)]
            pltpu.make_async_copy(w_slice, w_slice, w_sem.at[c, o, s]).wait()
            got = jnp.dot(h_v[s], w_slice[...], preferred_element_type=jnp.float32)

            @pl.when(s == 0)
            def _():
                out[...] = got

            @pl.when(s > 0)
            def _():
                out[...] = out[...] + got

            return carry

        lax.fori_loop(0, KS, step, 0)

    def produce(c, carry):
        for i in range(1, chunks):
            @pl.when(c == i - 1)
            def _():
                for o in range(2):
                    for s in range(KS):
                        w_copy(i, o, s).start()

        @pl.when(c == chunks - 2)
        def _():
            for i in range(chunks):
                cache_in(i).start()

        partial(c, 0, part_s.at[c], True)

        @pl.when(c == 0)
        def _():
            pl.semaphore_wait(barrier, n)

        swap = pltpu.make_async_remote_copy(
            src_ref=part_s.at[c],
            dst_ref=part_r.at[c],
            send_sem=ps_sem.at[c],
            recv_sem=pr_sem.at[c],
            device_id={"head": other},
            device_id_type=MESH,
        )
        swap.start()
        partial(c, 1, own_v, False)
        swap.wait()
        total = own_v[...] + part_r[c] + bias_v[c]
        cosine = cos_v[...]
        sine = sin_v[...]
        pieces = []
        for j in range(2):
            x = total[:, j * hd:(j + 1) * hd]
            pieces.append(x * cosine + pltpu.roll(x, hd // 2, 1) * sine)
        rounded = jnp.concatenate(pieces, axis=1).astype(jnp.bfloat16)
        placed = jnp.dot(p_v[...], rounded, preferred_element_type=jnp.float32)
        left = placed[:, :hd].reshape(n * cap, page, hd)
        right = placed[:, hd:].reshape(n * cap, page, hd)
        send_v[c] = jnp.concatenate([left, right], axis=1).astype(jnp.bfloat16)
        pltpu.make_async_copy(
            send_v.at[c, pl.ds(0, cap)], recv_v.at[c, pl.ds(0, cap)], l_sem.at[c]
        ).start()

        def send(j, carry2):
            k = n // 2 + (1 - 2 * (j % 2)) * ((j + 1) // 2)
            pltpu.make_async_remote_copy(
                src_ref=send_v.at[c, pl.ds(k * cap, cap)],
                dst_ref=recv_v.at[c, pl.ds(k * cap, cap)],
                send_sem=s_sem.at[c],
                recv_sem=r_sem.at[c],
                device_id={"seq": lax.rem(me + k, n)},
                device_id_type=MESH,
            ).start()
            return carry2

        lax.fori_loop(0, n - 1, send, 0)

        @pl.when(c == per - 1)
        def _():
            rope_table()

        return carry

    lax.fori_loop(0, chunks, produce, 0)

    unpack_table()
    head_lane = lax.broadcasted_iota(jnp.int32, (1, 1, hd), 2)
    written = (sr_v[...] >= 0.0)[: slots * page]

    def consume(c, carry):
        pltpu.make_async_copy(
            recv_v.at[c, pl.ds(0, cap)], recv_v.at[c, pl.ds(0, cap)], l_sem.at[c]
        ).wait()
        rest = recv_v.at[c, pl.ds(cap, (n - 1) * cap)]
        pltpu.make_async_copy(rest, rest, r_sem.at[c]).wait()
        pltpu.make_async_copy(cache_v.at[c], cache_v.at[c], c_sem.at[c]).wait()
        got = recv_v[c].astype(jnp.float32)
        coded = []
        for j in range(2):
            x = got[:, j * page:(j + 1) * page, :]
            largest = jnp.max(jnp.max(jnp.abs(x), axis=1, keepdims=True), axis=2, keepdims=True)
            scale = (largest + eps).astype(jnp.bfloat16).astype(jnp.float32)
            scale_v[...] += jnp.where(head_lane == 2 * c + j, scale, 0.0)
            coded.append((x / scale).reshape(n * cap * page, hd))
        codes = jnp.concatenate(coded, axis=1).astype(jnp.bfloat16)
        placed = jnp.dot(u_v[...], codes, preferred_element_type=jnp.float32)
        placed = placed[: slots * page]
        old = cache_v[c].astype(jnp.float32).reshape(slots * page, wide)
        cache_v[c] = (
            jnp.where(written, placed, old).reshape(slots, page, wide).astype(jnp.bfloat16)
        )
        for i in range(chunks):
            @pl.when(c == i)
            def _():
                cache_out(i).start()
        return carry

    lax.fori_loop(0, chunks, consume, 0)

    flat = jnp.broadcast_to(scale_v[...], (n * cap, page, hd)).reshape(n * cap * page, hd)
    spread = jnp.dot(u_v[...], flat.astype(jnp.bfloat16), preferred_element_type=jnp.float32)
    spread = spread[: slots * page].reshape(slots, page, hd)[:, 0, :]
    spread = jnp.concatenate([spread, jnp.zeros((128 - slots % 128, hd), f32)], axis=0)
    spread = jnp.transpose(spread)[:, :slots]
    vs_out[...] = jnp.where(
        spread[:heads] > 0.0, spread[:heads], ovs_ref[...].astype(f32)
    ).astype(jnp.bfloat16)
    ks_out[...] = jnp.where(
        spread[heads:2 * heads] > 0.0, spread[heads:2 * heads], oks_ref[...].astype(f32)
    ).astype(jnp.bfloat16)

    for c in range(chunks):
        cache_out(c).wait()
        out = send_v.at[c, pl.ds(cap, (n - 1) * cap)]
        pltpu.make_async_copy(out, out, s_sem.at[c]).wait()


def hand_on(pieces, *refs):
    srcs, dsts, held = refs[:4], refs[4:8], refs[8:12]
    in_sem, out_sem = refs[12:]
    views = []
    for src, dst, here in zip(srcs, dsts, held):
        if src.shape[0] >= 8:
            size = src.shape[0]
            cuts = [size * i // pieces for i in range(pieces + 1)]
            for low, high in zip(cuts, cuts[1:]):
                part = pl.ds(low, high - low)
                views.append((src.at[part], dst.at[part], here.at[part]))
        else:
            views.append((src, dst, here))
    ins = [pltpu.make_async_copy(v[0], v[2], in_sem.at[i]) for i, v in enumerate(views)]
    outs = [pltpu.make_async_copy(v[2], v[1], out_sem.at[i]) for i, v in enumerate(views)]
    for copy in ins:
        copy.start()
    for copy_in, copy_out in zip(ins, outs):
        copy_in.wait()
        copy_out.start()
    for copy in outs:
        copy.wait()


def shards(
    hidden,
    key_weight,
    value_weight,
    key_bias,
    value_bias,
    request_tokens,
    request_context,
    page_owner,
    page_slot,
    key_cache,
    value_cache,
    stored_key_scales,
    value_scales,
):
    toks, depth = hidden.shape
    slots, page, cols = key_cache.shape
    heads = stored_key_scales.shape[1]
    hd = cols // heads
    pages_here = toks // page
    n = lax.axis_size("seq")
    cap = (pages_here + n - 1) // n + 1
    half = hd // 2
    rows = n * cap * page
    srows = (slots * page + 15) // 16 * 16

    freqs = jnp.exp(
        -jnp.log(jnp.float32(rope_base)) * (2.0 * jnp.arange(half).astype(jnp.float32) / hd)
    )
    freqs = jnp.concatenate([freqs, freqs]).reshape(1, hd)
    wide = 2 * hd
    chunks = 2 * (cols // wide)
    vm = pl.BlockSpec(memory_space=pltpu.VMEM)
    hbm = pl.BlockSpec(memory_space=pl.ANY)
    f32, b16 = jnp.float32, jnp.bfloat16
    old_value_scales = value_scales
    done = pl.pallas_call(
        functools.partial(body, n, cap, heads, hd, page),
        out_shape=(
            jax.ShapeDtypeStruct(key_cache.shape, b16),
            jax.ShapeDtypeStruct(value_cache.shape, b16),
            jax.ShapeDtypeStruct((heads, slots), b16),
            jax.ShapeDtypeStruct((heads, slots), b16),
        ),
        in_specs=[hbm] * 14,
        out_specs=(hbm, hbm, vm, vm),
        scratch_shapes=[
            pltpu.VMEM((KS, toks, depth // KS), b16),
            pltpu.VMEM((chunks, 2, depth, wide), b16),
            pltpu.VMEM((rows, toks), b16),
            pltpu.VMEM((srows, rows), b16),
            pltpu.VMEM((chunks, toks, wide), f32),
            pltpu.VMEM((chunks, toks, wide), f32),
            pltpu.VMEM((toks, wide), f32),
            pltpu.VMEM((chunks, 1, wide), f32),
            pltpu.VMEM((chunks, n * cap, 2 * page, hd), b16),
            pltpu.VMEM((chunks, n * cap, 2 * page, hd), b16),
            pltpu.VMEM((chunks, slots, page, wide), b16),
            pltpu.VMEM((n * cap, 1, hd), f32),
            pltpu.VMEM((toks, hd), f32),
            pltpu.VMEM((toks, hd), f32),
            pltpu.VMEM((srows, 1), f32),
            pltpu.VMEM((1, page_owner.shape[0]), jnp.int32),
            pltpu.VMEM((1, page_owner.shape[0]), jnp.int32),
            pltpu.VMEM((1, hd), f32),
            pltpu.VMEM((1, cols), f32),
            pltpu.VMEM((1, cols), f32),
            pltpu.VMEM((heads, slots), b16),
            pltpu.VMEM((heads, slots), b16),
            pltpu.SMEM(request_tokens.shape, jnp.int32),
            pltpu.SMEM(request_tokens.shape, jnp.int32),
            pltpu.SemaphoreType.DMA((KS,)),
            pltpu.SemaphoreType.DMA((chunks, 2, KS)),
            pltpu.SemaphoreType.DMA((chunks,)),
            pltpu.SemaphoreType.DMA((chunks,)),
            pltpu.SemaphoreType.DMA((chunks,)),
            pltpu.SemaphoreType.DMA((chunks,)),
            pltpu.SemaphoreType.DMA((chunks,)),
            pltpu.SemaphoreType.DMA((chunks,)),
            pltpu.SemaphoreType.DMA((chunks,)),
            pltpu.SemaphoreType.DMA((9,)),
        ],
        compiler_params=pltpu.CompilerParams(
            collective_id=0, has_side_effects=True, vmem_limit_bytes=60 * 1024 * 1024
        ),
    )(
        page_owner.reshape(1, -1), page_slot.reshape(1, -1), freqs,
        key_bias.reshape(1, -1), value_bias.reshape(1, -1),
        stored_key_scales.T, old_value_scales.T, request_tokens, request_context,
        hidden, key_weight, value_weight, key_cache, value_cache,
    )
    pieces = 2
    moves = 2 * pieces + 2
    keys, values, key_scales, value_scales = pl.pallas_call(
        functools.partial(hand_on, pieces),
        out_shape=tuple(jax.ShapeDtypeStruct(a.shape, a.dtype) for a in done),
        in_specs=[hbm] * 4,
        out_specs=(hbm,) * 4,
        scratch_shapes=[pltpu.VMEM(a.shape, a.dtype) for a in done]
        + [pltpu.SemaphoreType.DMA((moves,)), pltpu.SemaphoreType.DMA((moves,))],
        compiler_params=pltpu.CompilerParams(vmem_limit_bytes=60 * 1024 * 1024),
    )(*done)
    return keys, values, key_scales.T, value_scales.T


def solution(mesh):
    placed = (
        P("seq", "head"),
        P("head", None),
        P("head", None),
        P("head"),
        P("head"),
        P(),
        P(),
        P(),
        P(),
        P("seq", None, "head"),
        P("seq", None, "head"),
        P("seq", "head"),
        P("seq", "head"),
    )
    return jax.shard_map(
        shards,
        mesh=mesh,
        in_specs=placed,
        out_specs=(
            P("seq", None, "head"),
            P("seq", None, "head"),
            P("seq", "head"),
            P("seq", "head"),
        ),
        check_vma=False,
    )
```

profile of v0, /device:TPU:0, one launch (start us, length us, event | category | flops | bytes accessed | tf_op | source)
XLA Modules:
  0.0 47.8 jit_solution(11324335472300998523)
XLA Ops:
  0.6 0.6 %maximum_bitcast_fusion.freq_in = f32[1,128]{1,0:T(1,128)} fusion(f32[64]{0:T(128)S(1)} %multiply_exponential_fusion), kind=kLoop, calls=%fused_computation | loop fusion | flops 128 | bytes 768 | tf_op jit(solution)/shard_map/reshape | solution.py:348
  1.2 44.5 %shard_map.156 = (bf16[79,8,512]{2,1,0:T(8,128)(2,1)}, bf16[79,8,512]{2,1,0:T(8,128)(2,1)}, bf16[4,79]{1,0:T(4,128)(2,1)}, bf16[4,79]{1,0:T(4,128)(2,1)}) custom-call(s32[1,1024]{1,0:T(1,128)} %bitcast.10, s32[1,1024]{1,0:T(1,128)} %bitcast.11, f32[1,128]{1,0:T(1,128)} %maximum_bitcast_fusion.freq_in, f32[1,512]{1,0:T(1,128)} %bitcast.12, ...), custom_call_target="tpu_custom_call" | custom-call | tf_op jit(solution)/shard_map/pallas_call | solution.py:355
  45.7 2.1 %shard_map.157 = (bf16[79,8,512]{2,1,0:T(8,128)(2,1)}, bf16[79,8,512]{2,1,0:T(8,128)(2,1)}, bf16[4,79]{1,0:T(4,128)(2,1)}, bf16[4,79]{1,0:T(4,128)(2,1)}) custom-call(bf16[79,8,512]{2,1,0:T(8,128)(2,1)} %get-tuple-element.12.refs_0_, bf16[79,8,512]{2,1,0:T(8,128)(2,1)} %get-tuple-element.13.refs_1_, bf16[4,79]{1,0:T(4,128)(2,1)} %get-tuple-element.14.refs_2_, ...), custom_call_target="tpu_custom_call" | custom-call | tf_op jit(solution)/shard_map/pallas_call | solution.py:412
  (1 shorter events, 0.0 us)
where the time goes:
time: 48 us; the launch traced here: 47.8 us
  Pallas kernels  46.6 us (97%)
  between operations  0.64 us (1%)
  other arithmetic  0.59 us (1%)
    pallas_call x1, Pallas kernels, shards(): pl.pallas_call(functools.partial(body, n, cap, heads, hd, page), out_shap...  44.5 us
    pallas_call x1, Pallas kernels, shards(): pl.pallas_call(functools.partial(hand_on, pieces), out_shape=tuple((jax.S...  2.12 us

commit v1 on v0

v1 whole, which is shorter than its diff:
```python
import functools
import math

import jax
import jax.numpy as jnp
from jax import lax
from jax.experimental import pallas as pl
from jax.experimental.pallas import tpu as pltpu
from jax.sharding import PartitionSpec as P

rope_base = 1000000.0
eps = 1e-06
KS = 4
MESH = pl.DeviceIdType.MESH


def body(
    n, cap, heads, hd, page, slots,
    own_in, slot_in, kb_in, vb_in, rt_in, rc_in,
    h_hbm, kw_hbm, vw_hbm, kc_hbm, vc_hbm,
    cache_v, spread_v,
    h_v, w_v, p_v, u_v, part_s, part_r, own_v, bias_v, send_v, recv_v, scale_v,
    cos_v, sin_v, sr_v,
    own_ref, slot_ref, kb_ref, vb_ref, rt_ref, rc_ref,
    h_sem, w0_sem, w_sem, c_sem, ps_sem, pr_sem, s_sem, r_sem, i_sem,
):
    toks, depth = h_v.shape
    kd = depth // KS
    chunks = 2 * heads
    half_cols = heads * hd
    f32, b16 = jnp.float32, jnp.bfloat16

    me = lax.axis_index("seq")
    side = lax.axis_index("head")
    other = 1 - side

    barrier = pltpu.get_barrier_semaphore()
    pl.semaphore_signal(barrier, inc=1, device_id={"head": other}, device_id_type=MESH)

    def greet(k, carry):
        pl.semaphore_signal(
            barrier, inc=1, device_id={"seq": lax.rem(me + k, n)}, device_id_type=MESH
        )
        return carry

    lax.fori_loop(1, n, greet, 0)

    def w_copies(c, rows, sem):
        src = vw_hbm if c < heads else kw_hbm
        copies = []
        for o, owner in enumerate((other, side)):
            col = pl.multiple_of(owner * half_cols + (c % heads) * hd, hd)
            copies.append(
                pltpu.make_async_copy(
                    src.at[rows, pl.ds(col, hd)], w_v.at[c, rows, pl.ds(o * hd, hd)], sem
                )
            )
        return copies

    def h_copy(s):
        part = pl.ds(s * kd, kd)
        return pltpu.make_async_copy(h_hbm.at[:, part], h_v.at[:, part], h_sem.at[s])

    pairs = (
        (own_in, own_ref), (slot_in, slot_ref), (kb_in, kb_ref),
        (vb_in, vb_ref), (rt_in, rt_ref), (rc_in, rc_ref),
    )
    small = [
        pltpu.make_async_copy(src, dst, i_sem.at[i]) for i, (src, dst) in enumerate(pairs)
    ]
    small[0].start()
    for s in range(KS):
        h_copy(s).start()
        for copy in w_copies(0, pl.ds(s * kd, kd), w0_sem.at[s]):
            copy.start()
    for copy in small[1:]:
        copy.start()
    for copy in w_copies(1, pl.ds(0, depth), w_sem.at[1]):
        copy.start()
    for copy in small:
        copy.wait()

    for c in range(chunks):
        src = vb_ref if c < heads else kb_ref
        bias_v[c] = src[:, pl.ds((c % heads) * hd, hd)]
    total_pages = own_ref.shape[1]
    here = total_pages // n
    owner = own_ref[...]
    gid = lax.broadcasted_iota(jnp.int32, (1, total_pages), 1)
    within = gid % here
    match = lax.broadcasted_iota(jnp.int32, (n, total_pages), 0) == owner
    count = jnp.where(match, 1.0, 0.0)
    shift = 1
    while shift < here:
        count = count + jnp.where(within >= shift, pltpu.roll(count, shift, 1), 0.0)
        shift *= 2
    rank = jnp.sum(jnp.where(match, count, 0.0), axis=0, keepdims=True) - 1.0
    place = ((owner - me + n) % n * cap).astype(f32) + rank
    place = pltpu.roll(
        jnp.broadcast_to(place, (8, total_pages)), (total_pages - me * here) % total_pages, 1
    )[:, :here]
    expand = (
        lax.broadcasted_iota(jnp.int32, (here, toks), 0)
        == lax.broadcasted_iota(jnp.int32, (here, toks), 1) // page
    )
    place = jnp.dot(
        place.astype(b16),
        jnp.where(expand, 1.0, 0.0).astype(b16),
        preferred_element_type=f32,
    )[:1]
    token = lax.broadcasted_iota(jnp.int32, (1, toks), 1)
    dk = place * page + (token % page).astype(f32)
    rows = lax.broadcasted_iota(jnp.int32, p_v.shape, 0).astype(f32)
    p_v[...] = jnp.where(rows == dk, 1.0, 0.0).astype(b16)

    def unpack_table():
        slot = jnp.where(owner == me, slot_ref[...], -1)
        lane = (((me - gid // here + n) % n) * cap).astype(f32) + rank + 1.0
        want = lax.broadcasted_iota(jnp.int32, (u_v.shape[0], 1), 0)
        src = jnp.sum(jnp.where(want // page == slot, lane, 0.0), axis=1, keepdims=True) - 1.0
        sr_v[...] = jnp.where(src >= 0.0, src * page + (want % page).astype(f32), -1.0)
        lanes = lax.broadcasted_iota(jnp.int32, u_v.shape, 1).astype(f32)
        u_v[...] = jnp.where(lanes == sr_v[...], 1.0, 0.0).astype(b16)

    def rope_table():
        half = hd // 2
        lane = (lax.broadcasted_iota(jnp.int32, (1, hd), 1) % half).astype(f32)
        freq = jnp.exp(-jnp.float32(math.log(rope_base)) * (2.0 * lane / hd))
        token_ids = me * toks + lax.broadcasted_iota(jnp.int32, cos_v.shape, 0)
        offset = jnp.zeros_like(token_ids)
        start = jnp.int32(0)
        for r in range(rt_ref.shape[0]):
            offset = jnp.where(token_ids >= start, rc_ref[r] - start, offset)
            start = start + rt_ref[r]
        angle = (offset + token_ids).astype(f32) * freq
        cos_v[...] = jnp.cos(angle)
        sine = jnp.sin(angle)
        front = lax.broadcasted_iota(jnp.int32, cos_v.shape, 1) < half
        sin_v[...] = jnp.where(front, -sine, sine)

    cos_v[...] = jnp.ones_like(cos_v)
    sin_v[...] = jnp.zeros_like(sin_v)
    scale_v[...] = jnp.zeros_like(scale_v)

    def swap(c):
        return pltpu.make_async_remote_copy(
            src_ref=part_s.at[c],
            dst_ref=part_r.at[c],
            send_sem=ps_sem.at[c],
            recv_sem=pr_sem.at[c],
            device_id={"head": other},
            device_id_type=MESH,
        )

    def post(c):
        swap(c).wait()
        x = own_v[c % 2] + part_r[c] + bias_v[c]
        x = x * cos_v[...] + pltpu.roll(x, hd // 2, 1) * sin_v[...]
        placed = jnp.dot(p_v[...], x.astype(b16), preferred_element_type=f32)
        placed = placed.reshape(n * cap, page, hd).astype(b16)
        send_v[c] = placed
        recv_v[c, :cap] = placed[:cap]

        def send(k, carry):
            pltpu.make_async_remote_copy(
                src_ref=send_v.at[c, pl.ds(k * cap, cap)],
                dst_ref=recv_v.at[c, pl.ds(k * cap, cap)],
                send_sem=s_sem.at[c],
                recv_sem=r_sem.at[c],
                device_id={"seq": lax.rem(me + k, n)},
                device_id_type=MESH,
            ).start()
            return carry

        lax.fori_loop(1, n, send, 0)

    def first(s, carry):
        part = pl.ds(pl.multiple_of(s * kd, kd), kd)
        h_part = h_v.at[:, part]
        w_part = w_v.at[0, part]
        pltpu.make_async_copy(h_part, h_part, h_sem.at[s]).wait()
        pltpu.make_async_copy(w_part, w_part, w0_sem.at[s]).wait()
        got = jnp.dot(h_part[...], w_part[...], preferred_element_type=f32)

        @pl.when(s == 0)
        def _():
            part_s[0] = got[:, :hd]
            own_v[0] = got[:, hd:]

        @pl.when(s > 0)
        def _():
            part_s[0] = part_s[0] + got[:, :hd]
            own_v[0] = own_v[0] + got[:, hd:]

        return carry

    lax.fori_loop(0, KS, first, 0)
    for copy in w_copies(2, pl.ds(0, depth), w_sem.at[2]):
        copy.start()
    pl.semaphore_wait(barrier, n)
    swap(0).start()

    def produce(c, carry):
        for i in range(3, chunks):
            @pl.when(c == i - 2)
            def _():
                for copy in w_copies(i, pl.ds(0, depth), w_sem.at[i]):
                    copy.start()

        @pl.when(c == chunks - 2)
        def _():
            pltpu.make_async_copy(vc_hbm, cache_v.at[0], c_sem.at[0]).start()
            pltpu.make_async_copy(kc_hbm, cache_v.at[1], c_sem.at[1]).start()

        w_all = w_v.at[c]
        pltpu.make_async_copy(w_all, w_all, w_sem.at[c]).wait()
        got = jnp.dot(h_v[...], w_all[...], preferred_element_type=f32)
        part_s[c] = got[:, :hd]
        own_v[c % 2] = got[:, hd:]
        swap(c).start()
        post(c - 1)

        @pl.when(c == heads)
        def _():
            rope_table()

        return carry

    lax.fori_loop(1, chunks, produce, 0)
    post(chunks - 1)

    unpack_table()
    head_lane = lax.broadcasted_iota(jnp.int32, (1, 1, hd), 2)
    written = (sr_v[...] >= 0.0)[: slots * page]
    for i in range(2):
        pltpu.make_async_copy(cache_v.at[i], cache_v.at[i], c_sem.at[i]).wait()

    def consume(c, carry):
        rest = recv_v.at[c, pl.ds(cap, (n - 1) * cap)]
        pltpu.make_async_copy(rest, rest, r_sem.at[c]).wait()
        x = recv_v[c].astype(f32)
        largest = jnp.max(jnp.max(jnp.abs(x), axis=1, keepdims=True), axis=2, keepdims=True)
        scale = (largest + eps).astype(b16).astype(f32)
        scales = scale_v[...] + jnp.where(head_lane == c, scale, 0.0)
        scale_v[...] = scales
        codes = (x / scale).reshape(n * cap * page, hd)
        flat = jnp.broadcast_to(scales, (n * cap, page, hd)).reshape(n * cap * page, hd)
        both = jnp.concatenate([codes, flat], axis=1).astype(b16)
        placed = jnp.dot(u_v[...], both, preferred_element_type=f32)
        spread_v[...] = placed[:, hd:]
        lanes = pl.ds(pl.multiple_of((c % heads) * hd, hd), hd)
        old = cache_v[c // heads, :, :, lanes].astype(f32).reshape(slots * page, hd)
        new = jnp.where(written, placed[: slots * page, :hd], old)
        cache_v[c // heads, :, :, lanes] = new.reshape(slots, page, hd).astype(b16)
        return carry

    lax.fori_loop(0, chunks, consume, 0)

    for c in range(chunks):
        out = send_v.at[c, pl.ds(cap, (n - 1) * cap)]
        pltpu.make_async_copy(out, out, s_sem.at[c]).wait()


def hand_on(
    heads, page, slots,
    cache_v, spread_ref, oks_ref, ovs_ref,
    kc_out, vc_out, ks_out, vs_out,
    ks_v, vs_v, o_sem,
):
    f32 = jnp.float32
    copies = [
        pltpu.make_async_copy(cache_v.at[0], vc_out, o_sem.at[0]),
        pltpu.make_async_copy(cache_v.at[1], kc_out, o_sem.at[1]),
        pltpu.make_async_copy(vs_v, vs_out, o_sem.at[2]),
        pltpu.make_async_copy(ks_v, ks_out, o_sem.at[3]),
    ]
    for copy in copies[:2]:
        copy.start()
    hd = spread_ref.shape[1]
    spread = spread_ref[...][: slots * page].reshape(slots, page, hd)[:, 0, :]
    spread = jnp.concatenate([spread, jnp.zeros((128 - slots % 128, hd), f32)], axis=0)
    spread = jnp.transpose(spread)[:, :slots]
    vs_v[...] = jnp.where(
        spread[:heads] > 0.0, spread[:heads], ovs_ref[...].astype(f32)
    ).astype(jnp.bfloat16)
    ks_v[...] = jnp.where(
        spread[heads:2 * heads] > 0.0, spread[heads:2 * heads], oks_ref[...].astype(f32)
    ).astype(jnp.bfloat16)
    for copy in copies[2:]:
        copy.start()
    for copy in copies:
        copy.wait()


def shards(
    hidden,
    key_weight,
    value_weight,
    key_bias,
    value_bias,
    request_tokens,
    request_context,
    page_owner,
    page_slot,
    key_cache,
    value_cache,
    stored_key_scales,
    value_scales,
):
    toks, depth = hidden.shape
    slots, page, cols = key_cache.shape
    heads = stored_key_scales.shape[1]
    hd = cols // heads
    pages_here = toks // page
    n = lax.axis_size("seq")
    cap = (pages_here + n - 1) // n + 1
    rows = n * cap * page
    srows = (slots * page + 15) // 16 * 16
    chunks = 2 * heads
    vm = pl.BlockSpec(memory_space=pltpu.VMEM)
    hbm = pl.BlockSpec(memory_space=pl.ANY)
    f32, b16 = jnp.float32, jnp.bfloat16
    cache, spread = pl.pallas_call(
        functools.partial(body, n, cap, heads, hd, page, slots),
        out_shape=(
            pltpu.VMEM((2, slots, page, cols), b16),
            pltpu.VMEM((srows, hd), f32),
        ),
        in_specs=[hbm] * 11,
        out_specs=(vm, vm),
        scratch_shapes=[
            pltpu.VMEM((toks, depth), b16),
            pltpu.VMEM((chunks, depth, 2 * hd), b16),
            pltpu.VMEM((rows, toks), b16),
            pltpu.VMEM((srows, rows), b16),
            pltpu.VMEM((chunks, toks, hd), f32),
            pltpu.VMEM((chunks, toks, hd), f32),
            pltpu.VMEM((2, toks, hd), f32),
            pltpu.VMEM((chunks, 1, hd), f32),
            pltpu.VMEM((chunks, n * cap, page, hd), b16),
            pltpu.VMEM((chunks, n * cap, page, hd), b16),
            pltpu.VMEM((n * cap, 1, hd), f32),
            pltpu.VMEM((toks, hd), f32),
            pltpu.VMEM((toks, hd), f32),
            pltpu.VMEM((srows, 1), f32),
            pltpu.VMEM((1, page_owner.shape[0]), jnp.int32),
            pltpu.VMEM((1, page_owner.shape[0]), jnp.int32),
            pltpu.VMEM((1, cols), f32),
            pltpu.VMEM((1, cols), f32),
            pltpu.SMEM(request_tokens.shape, jnp.int32),
            pltpu.SMEM(request_tokens.shape, jnp.int32),
            pltpu.SemaphoreType.DMA((KS,)),
            pltpu.SemaphoreType.DMA((KS,)),
            pltpu.SemaphoreType.DMA((chunks,)),
            pltpu.SemaphoreType.DMA((2,)),
            pltpu.SemaphoreType.DMA((chunks,)),
            pltpu.SemaphoreType.DMA((chunks,)),
            pltpu.SemaphoreType.DMA((chunks,)),
            pltpu.SemaphoreType.DMA((chunks,)),
            pltpu.SemaphoreType.DMA((6,)),
        ],
        compiler_params=pltpu.CompilerParams(
            collective_id=0, has_side_effects=True, vmem_limit_bytes=48 * 1024 * 1024
        ),
    )(*[
        pltpu.with_memory_space_constraint(a, pltpu.HBM)
        for a in (
            page_owner.reshape(1, -1), page_slot.reshape(1, -1),
            key_bias.reshape(1, -1), value_bias.reshape(1, -1),
            request_tokens, request_context,
            hidden, key_weight, value_weight, key_cache, value_cache,
        )
    ])
    keys, values, key_scales, new_value_scales = pl.pallas_call(
        functools.partial(hand_on, heads, page, slots),
        out_shape=(
            jax.ShapeDtypeStruct(key_cache.shape, b16),
            jax.ShapeDtypeStruct(value_cache.shape, b16),
            jax.ShapeDtypeStruct((heads, slots), b16),
            jax.ShapeDtypeStruct((heads, slots), b16),
        ),
        in_specs=[vm] * 4,
        out_specs=(hbm,) * 4,
        scratch_shapes=[
            pltpu.VMEM((heads, slots), b16),
            pltpu.VMEM((heads, slots), b16),
            pltpu.SemaphoreType.DMA((4,)),
        ],
        compiler_params=pltpu.CompilerParams(vmem_limit_bytes=4 * 1024 * 1024),
    )(cache, spread, stored_key_scales.T, value_scales.T)
    return keys, values, key_scales.T, new_value_scales.T


def solution(mesh):
    placed = (
        P("seq", "head"),
        P("head", None),
        P("head", None),
        P("head"),
        P("head"),
        P(),
        P(),
        P(),
        P(),
        P("seq", None, "head"),
        P("seq", None, "head"),
        P("seq", "head"),
        P("seq", "head"),
    )
    return jax.shard_map(
        shards,
        mesh=mesh,
        in_specs=placed,
        out_specs=(
            P("seq", None, "head"),
            P("seq", None, "head"),
            P("seq", "head"),
            P("seq", "head"),
        ),
        check_vma=False,
    )
```

time: 48 us -> 44.2 us (0.921)
  Pallas kernels: 46.6 us -> 43.4 us
  other arithmetic: 0.59 us -> 0 us
    pallas_call x2, Pallas kernels: 46.6 us -> 43.4 us  [the longest x1 42.3 us: shards(): pl.pallas_call(functools.partial(body, n, cap, heads, hd, page, slots), o...]
    reshape x1 -> x0, other arithmetic: 0.59 us -> none  [shards(): freqs = jnp.concatenate([freqs, freqs]).reshape(1, hd)]
where the time goes in v1:
time: 44.2 us; the launch traced here: 44.1 us
  Pallas kernels  43.4 us (98%)
  between operations  0.68 us (2%)
    pallas_call x1, Pallas kernels, shards(): pl.pallas_call(functools.partial(body, n, cap, heads, hd, page, slots), o...  42.3 us
    pallas_call x1, Pallas kernels, shards(): pl.pallas_call(functools.partial(hand_on, heads, page, slots), out_shape=...  1.09 us

profile of v1, /device:TPU:0, one launch (start us, length us, event | category | flops | bytes accessed | tf_op | source)
XLA Modules:
  0.0 44.1 jit_solution(13470700206170975814)
XLA Ops:
  0.6 0.0 copy-start
  0.6 0.0 copy-start.1
  0.7 42.3 %shard_map.156 = (bf16[2,79,8,512]{3,2,1,0:T(8,128)(2,1)S(1)}, f32[640,128]{1,0:T(8,128)S(1)}) custom-call(s32[1,1024]{1,0:T(1,128)} %bitcast.10, s32[1,1024]{1,0:T(1,128)} %bitcast.11, f32[1,512]{1,0:T(1,128)} %bitcast.12, f32[1,512]{1,0:T(1,128)} %bitcast.13, s32[16]{0:T(128)} %rt_in.1, s32[16]{0:T(128)} %rc_in.1, bf16[512,4096]{1,0:T(8,128)(2,1)} %h_hbm.1, ...), custom_call_target="tpu_custom_call" | custom-call | tf_op jit(solution)/shard_map/pallas_call | solution.py:323
  43.0 0.0 copy-done
  43.0 0.0 copy-done.1
  43.0 1.1 %shard_map.157 = (bf16[79,8,512]{2,1,0:T(8,128)(2,1)}, bf16[79,8,512]{2,1,0:T(8,128)(2,1)}, bf16[4,79]{1,0:T(4,128)(2,1)}, bf16[4,79]{1,0:T(4,128)(2,1)}) custom-call(bf16[2,79,8,512]{3,2,1,0:T(8,128)(2,1)S(1)} %get-tuple-element.10.cache_v, f32[640,128]{1,0:T(8,128)S(1)} %get-tuple-element.11.spread_ref, bf16[4,79]{1,0:T(4,128)(2,1)S(1)} %bitcast.8, ...), custom_call_target="tpu_custom_call" | custom-call | tf_op jit(solution)/shard_map/pallas_call | solution.py:374
Async XLA Ops:
  0.6 42.3 %copy-start = (bf16[79,4]{0,1:T(4,128)(2,1)S(1)}, bf16[79,4]{0,1:T(4,128)(2,1)}, u32[]{:S(2)}) copy-start(bf16[79,4]{0,1:T(4,128)(2,1)} %param.24) | copy-start | bytes 1900
  0.6 42.3 %copy-start.1 = (bf16[79,4]{0,1:T(4,128)(2,1)S(1)}, bf16[79,4]{0,1:T(4,128)(2,1)}, u32[]{:S(2)}) copy-start(bf16[79,4]{0,1:T(4,128)(2,1)} %param.25) | copy-start | bytes 1900

commit v2 on v1

v2 whole, which is shorter than its diff:
```python
import functools
import math

import jax
import jax.numpy as jnp
from jax import lax
from jax.experimental import pallas as pl
from jax.experimental.pallas import tpu as pltpu
from jax.sharding import PartitionSpec as P

rope_base = 1000000.0
eps = 1e-06
KS = 4
LATE = 3
MESH = pl.DeviceIdType.MESH


def groups_of(chunks):
    edges = [0, 1] + list(range(2, chunks - 2, 2)) + [chunks - 2, chunks - 1, chunks]
    return tuple(zip(edges, edges[1:]))


def coded(c, x, scales):
    count, page, hd = x.shape
    lane = lax.broadcasted_iota(jnp.int32, (1, 1, hd), 2)
    x = x.astype(jnp.float32)
    largest = jnp.max(jnp.max(jnp.abs(x), axis=1, keepdims=True), axis=2, keepdims=True)
    scale = (largest + eps).astype(jnp.bfloat16).astype(jnp.float32)
    codes = (x / scale).reshape(count * page, hd)
    return codes, scales + jnp.where(lane == c, scale, 0.0)


def body(
    n, cap, heads, hd, page, slots,
    own_in, slot_in, kb_in, vb_in, rt_in, rc_in,
    h_hbm, kw_hbm, vw_hbm, kc_hbm, vc_hbm,
    cache_v, last_v, u_v, sr_v, scale_v,
    h_v, w_v, p_v, part_s, part_r, own_v, bias_v, send_v, recv_v,
    cos_v, sin_v,
    own_ref, slot_ref, kb_ref, vb_ref, rt_ref, rc_ref,
    h_sem, w0_sem, w_sem, c_sem, ps_sem, pr_sem, s_sem, r_sem, i_sem,
):
    toks, depth = h_v.shape
    kd = depth // KS
    chunks = 2 * heads
    groups = groups_of(chunks)
    half_cols = heads * hd
    f32, b16 = jnp.float32, jnp.bfloat16

    me = lax.axis_index("seq")
    side = lax.axis_index("head")
    other = 1 - side

    def w_copy(c, o, rows, sem):
        src = vw_hbm if c < heads else kw_hbm
        owner = side if o else other
        col = pl.multiple_of(owner * half_cols + (c % heads) * hd, hd)
        return pltpu.make_async_copy(
            src.at[rows, pl.ds(col, hd)], w_v.at[c, rows, pl.ds(o * hd, hd)], sem
        )

    def w_start(c):
        for o in range(2):
            w_copy(c, o, pl.ds(0, depth), w_sem.at[c]).start()

    def h_copy(s):
        part = pl.ds(s * kd, kd)
        return pltpu.make_async_copy(h_hbm.at[:, part], h_v.at[:, part], h_sem.at[s])

    pairs = (
        (own_in, own_ref), (slot_in, slot_ref), (kb_in, kb_ref),
        (vb_in, vb_ref), (rt_in, rt_ref), (rc_in, rc_ref),
    )
    small = [
        pltpu.make_async_copy(src, dst, i_sem.at[i]) for i, (src, dst) in enumerate(pairs)
    ]
    small[0].start()
    for s in range(KS):
        h_copy(s).start()
        for o in range(2):
            w_copy(0, o, pl.ds(s * kd, kd), w0_sem.at[s]).start()

    barrier = pltpu.get_barrier_semaphore()
    pl.semaphore_signal(barrier, inc=1, device_id={"head": other}, device_id_type=MESH)

    def greet(k, carry):
        pl.semaphore_signal(
            barrier, inc=1, device_id={"seq": lax.rem(me + k, n)}, device_id_type=MESH
        )
        return carry

    lax.fori_loop(1, n, greet, 0)
    for copy in small[1:]:
        copy.start()
    w_start(1)

    def rope_table():
        half = hd // 2
        lane = (lax.broadcasted_iota(jnp.int32, (1, hd), 1) % half).astype(f32)
        freq = jnp.exp(-jnp.float32(math.log(rope_base)) * (2.0 * lane / hd))
        token_ids = me * toks + lax.broadcasted_iota(jnp.int32, cos_v.shape, 0)
        offset = jnp.zeros_like(token_ids)
        start = jnp.int32(0)
        for r in range(rt_ref.shape[0]):
            offset = jnp.where(token_ids >= start, rc_ref[r] - start, offset)
            start = start + rt_ref[r]
        angle = (offset + token_ids).astype(f32) * freq
        cos_v[...] = jnp.cos(angle)
        sine = jnp.sin(angle)
        front = lax.broadcasted_iota(jnp.int32, cos_v.shape, 1) < half
        sin_v[...] = jnp.where(front, -sine, sine)

    def swap(c):
        return pltpu.make_async_remote_copy(
            src_ref=part_s.at[c],
            dst_ref=part_r.at[c],
            send_sem=ps_sem.at[c],
            recv_sem=pr_sem.at[c],
            device_id={"head": other},
            device_id_type=MESH,
        )

    def launch(g, wanted):
        low, high = groups[g]
        part = pl.ds(low, high - low)

        def send(i, carry):
            there, spot = i // 4, (me + i) % 4
            dest = there * 4 + spot
            k = lax.rem(dest - me + n, n)
            steps = spot % 2 + spot // 2 + there % 2
            pick = dest != me
            if wanted is not None:
                pick = jnp.logical_and(pick, wanted(steps))

            @pl.when(pick)
            def _():
                pltpu.make_async_remote_copy(
                    src_ref=send_v.at[part, pl.ds(k * cap, cap)],
                    dst_ref=recv_v.at[part, pl.ds(k * cap, cap)],
                    send_sem=s_sem.at[g],
                    recv_sem=r_sem.at[g],
                    device_id={"seq": dest},
                    device_id_type=MESH,
                ).start()

            return carry

        lax.fori_loop(0, n, send, 0)

    def launches(g):
        late = len(groups) - LATE
        if g < late:
            launch(g, None)
            return
        launch(g, lambda steps: steps <= 1)
        if g == len(groups) - 1:
            for e in range(late, g):
                launch(e, lambda steps: steps > 1)
            launch(g, lambda steps: steps > 1)

    def post(c):
        swap(c).wait()
        x = own_v[c % 2] + part_r[c] + bias_v[c]
        x = x * cos_v[...] + pltpu.roll(x, hd // 2, 1) * sin_v[...]
        placed = jnp.dot(p_v[...], x.astype(b16), preferred_element_type=f32)
        placed = placed.reshape(n * cap, page, hd).astype(b16)
        send_v[c] = placed
        recv_v[c, :cap] = placed[:cap]
        for g, (low, high) in enumerate(groups):
            if isinstance(c, int):
                if high == c + 1:
                    launches(g)
            else:
                @pl.when(c == high - 1)
                def _():
                    launches(g)

    def first(s, carry):
        part = pl.ds(pl.multiple_of(s * kd, kd), kd)
        h_part = h_v.at[:, part]
        w_part = w_v.at[0, part]
        pltpu.make_async_copy(h_part, h_part, h_sem.at[s]).wait()
        pltpu.make_async_copy(w_part, w_part, w0_sem.at[s]).wait()
        got = jnp.dot(h_part[...], w_part[...], preferred_element_type=f32)

        @pl.when(s == 0)
        def _():
            part_s[0] = got[:, :hd]
            own_v[0] = got[:, hd:]

        @pl.when(s > 0)
        def _():
            part_s[0] = part_s[0] + got[:, :hd]
            own_v[0] = own_v[0] + got[:, hd:]

        return carry

    lax.fori_loop(0, KS, first, 0)
    w_start(2)
    pl.semaphore_wait(barrier, n)
    swap(0).start()
    small[0].wait()

    total_pages = own_ref.shape[1]
    here = total_pages // n
    owner = own_ref[...]
    gid = lax.broadcasted_iota(jnp.int32, (1, total_pages), 1)
    within = gid % here
    match = lax.broadcasted_iota(jnp.int32, (n, total_pages), 0) == owner
    count = jnp.where(match, 1.0, 0.0)
    shift = 1
    while shift < here:
        count = count + jnp.where(within >= shift, pltpu.roll(count, shift, 1), 0.0)
        shift *= 2
    rank = jnp.sum(jnp.where(match, count, 0.0), axis=0, keepdims=True) - 1.0
    place = ((owner - me + n) % n * cap).astype(f32) + rank
    place = pltpu.roll(
        jnp.broadcast_to(place, (8, total_pages)), (total_pages - me * here) % total_pages, 1
    )[:, :here]
    expand = (
        lax.broadcasted_iota(jnp.int32, (here, toks), 0)
        == lax.broadcasted_iota(jnp.int32, (here, toks), 1) // page
    )
    place = jnp.dot(
        place.astype(b16),
        jnp.where(expand, 1.0, 0.0).astype(b16),
        preferred_element_type=f32,
    )[:1]
    token = lax.broadcasted_iota(jnp.int32, (1, toks), 1)
    dk = place * page + (token % page).astype(f32)
    rows = lax.broadcasted_iota(jnp.int32, p_v.shape, 0).astype(f32)
    p_v[...] = jnp.where(rows == dk, 1.0, 0.0).astype(b16)

    cos_v[...] = jnp.ones_like(cos_v)
    sin_v[...] = jnp.zeros_like(sin_v)
    scale_v[...] = jnp.zeros_like(scale_v)

    def unpack_table():
        slot = jnp.where(owner == me, slot_ref[...], -1)
        lane = (((me - gid // here + n) % n) * cap).astype(f32) + rank + 1.0
        want = lax.broadcasted_iota(jnp.int32, (u_v.shape[0], 1), 0)
        src = jnp.sum(jnp.where(want // page == slot, lane, 0.0), axis=1, keepdims=True) - 1.0
        sr_v[...] = jnp.where(src >= 0.0, src * page + (want % page).astype(f32), -1.0)
        lanes = lax.broadcasted_iota(jnp.int32, u_v.shape, 1).astype(f32)
        u_v[...] = jnp.where(lanes == sr_v[...], 1.0, 0.0).astype(b16)

    for copy in small[1:]:
        copy.wait()
    for c in range(chunks):
        src = vb_ref if c < heads else kb_ref
        bias_v[c] = src[:, pl.ds((c % heads) * hd, hd)]
    post(0)

    def produce(c, carry):
        for i in range(3, chunks):
            @pl.when(c == i - 2)
            def _():
                w_start(i)

        @pl.when(c == chunks - 2)
        def _():
            pltpu.make_async_copy(vc_hbm, cache_v.at[0], c_sem.at[0]).start()
            pltpu.make_async_copy(kc_hbm, cache_v.at[1], c_sem.at[1]).start()

        w_all = w_v.at[c]
        pltpu.make_async_copy(w_all, w_all, w_sem.at[c]).wait()
        got = jnp.dot(h_v[...], w_all[...], preferred_element_type=f32)
        part_s[c] = got[:, :hd]
        own_v[c % 2] = got[:, hd:]
        swap(c).start()

        @pl.when(c > 1)
        def _():
            post(c - 1)

        @pl.when(c == heads)
        def _():
            rope_table()

        return carry

    lax.fori_loop(1, chunks, produce, 0)
    post(chunks - 1)

    unpack_table()
    written = (sr_v[...] >= 0.0)[: slots * page]
    for i in range(2):
        pltpu.make_async_copy(cache_v.at[i], cache_v.at[i], c_sem.at[i]).wait()

    def receive(c, carry):
        for g, (low, high) in enumerate(groups):
            @pl.when(c == low)
            def _():
                rest = recv_v.at[pl.ds(low, high - low), pl.ds(cap, (n - 1) * cap)]
                pltpu.make_async_copy(rest, rest, r_sem.at[g]).wait()

        @pl.when(c < chunks - 1)
        def _():
            codes, scale_v[...] = coded(c, recv_v[c], scale_v[...])
            placed = jnp.dot(u_v[...], codes.astype(b16), preferred_element_type=f32)
            lanes = pl.ds(pl.multiple_of((c % heads) * hd, hd), hd)
            old = cache_v[c // heads, :, :, lanes].astype(f32).reshape(slots * page, hd)
            new = jnp.where(written, placed[: slots * page], old)
            cache_v[c // heads, :, :, lanes] = new.reshape(slots, page, hd).astype(b16)

        return carry

    lax.fori_loop(0, chunks, receive, 0)
    last_v[...] = recv_v[chunks - 1]

    for g, (low, high) in enumerate(groups):
        out = send_v.at[pl.ds(low, high - low), pl.ds(cap, (n - 1) * cap)]
        pltpu.make_async_copy(out, out, s_sem.at[g]).wait()


def hand_on(
    heads, hd,
    held_v, last_v, u_v, sr_v, held_scale, oks_ref, ovs_ref,
    kc_out, vc_out, ks_out, vs_out,
    tail_v, ks_v, vs_v, o_sem,
):
    f32, b16 = jnp.float32, jnp.bfloat16
    slots, page = held_v.shape[1:3]
    cut = (heads - 1) * hd
    copies = [
        pltpu.make_async_copy(held_v.at[0], vc_out, o_sem.at[0]),
        pltpu.make_async_copy(
            held_v.at[1, :, :, pl.ds(0, cut)], kc_out.at[:, :, pl.ds(0, cut)], o_sem.at[1]
        ),
        pltpu.make_async_copy(tail_v, kc_out.at[:, :, pl.ds(cut, hd)], o_sem.at[2]),
        pltpu.make_async_copy(vs_v, vs_out, o_sem.at[3]),
        pltpu.make_async_copy(ks_v, ks_out, o_sem.at[4]),
    ]
    for copy in copies[:2]:
        copy.start()
    count = last_v.shape[0]
    codes, scales = coded(2 * heads - 1, last_v[...], held_scale[...])
    flat = jnp.broadcast_to(scales, (count, page, hd)).reshape(count * page, hd)
    both = jnp.concatenate([codes, flat], axis=1).astype(b16)
    placed = jnp.dot(u_v[...], both, preferred_element_type=f32)[: slots * page]
    written = (sr_v[...] >= 0.0)[: slots * page]
    old = held_v[1, :, :, cut:].astype(f32).reshape(slots * page, hd)
    new = jnp.where(written, placed[:, :hd], old)
    tail_v[...] = new.reshape(slots, page, hd).astype(b16)
    copies[2].start()
    spread = placed[:, hd:].reshape(slots, page, hd)[:, 0, :]
    spread = jnp.concatenate([spread, jnp.zeros((128 - slots % 128, hd), f32)], axis=0)
    spread = jnp.transpose(spread)[:, :slots]
    vs_v[...] = jnp.where(spread[:heads] > 0.0, spread[:heads], ovs_ref[...].astype(f32)).astype(b16)
    ks_v[...] = jnp.where(
        spread[heads:2 * heads] > 0.0, spread[heads:2 * heads], oks_ref[...].astype(f32)
    ).astype(b16)
    for copy in copies[3:]:
        copy.start()
    for copy in copies:
        copy.wait()


def shards(
    hidden,
    key_weight,
    value_weight,
    key_bias,
    value_bias,
    request_tokens,
    request_context,
    page_owner,
    page_slot,
    key_cache,
    value_cache,
    stored_key_scales,
    value_scales,
):
    toks, depth = hidden.shape
    slots, page, cols = key_cache.shape
    heads = stored_key_scales.shape[1]
    hd = cols // heads
    pages_here = toks // page
    n = lax.axis_size("seq")
    cap = (pages_here + n - 1) // n + 1
    rows = n * cap * page
    srows = (slots * page + 15) // 16 * 16
    chunks = 2 * heads
    groups = groups_of(chunks)
    vm = pl.BlockSpec(memory_space=pltpu.VMEM)
    hbm = pl.BlockSpec(memory_space=pl.ANY)
    f32, b16 = jnp.float32, jnp.bfloat16
    held = pl.pallas_call(
        functools.partial(body, n, cap, heads, hd, page, slots),
        out_shape=(
            pltpu.VMEM((2, slots, page, cols), b16),
            pltpu.VMEM((n * cap, page, hd), b16),
            pltpu.VMEM((srows, rows), b16),
            pltpu.VMEM((srows, 1), f32),
            pltpu.VMEM((n * cap, 1, hd), f32),
        ),
        in_specs=[hbm] * 11,
        out_specs=(vm,) * 5,
        scratch_shapes=[
            pltpu.VMEM((toks, depth), b16),
            pltpu.VMEM((chunks, depth, 2 * hd), b16),
            pltpu.VMEM((rows, toks), b16),
            pltpu.VMEM((chunks, toks, hd), f32),
            pltpu.VMEM((chunks, toks, hd), f32),
            pltpu.VMEM((2, toks, hd), f32),
            pltpu.VMEM((chunks, 1, hd), f32),
            pltpu.VMEM((chunks, n * cap, page, hd), b16),
            pltpu.VMEM((chunks, n * cap, page, hd), b16),
            pltpu.VMEM((toks, hd), f32),
            pltpu.VMEM((toks, hd), f32),
            pltpu.VMEM((1, page_owner.shape[0]), jnp.int32),
            pltpu.VMEM((1, page_owner.shape[0]), jnp.int32),
            pltpu.VMEM((1, cols), f32),
            pltpu.VMEM((1, cols), f32),
            pltpu.SMEM(request_tokens.shape, jnp.int32),
            pltpu.SMEM(request_tokens.shape, jnp.int32),
            pltpu.SemaphoreType.DMA((KS,)),
            pltpu.SemaphoreType.DMA((KS,)),
            pltpu.SemaphoreType.DMA((chunks,)),
            pltpu.SemaphoreType.DMA((2,)),
            pltpu.SemaphoreType.DMA((chunks,)),
            pltpu.SemaphoreType.DMA((chunks,)),
            pltpu.SemaphoreType.DMA((len(groups),)),
            pltpu.SemaphoreType.DMA((len(groups),)),
            pltpu.SemaphoreType.DMA((6,)),
        ],
        compiler_params=pltpu.CompilerParams(
            collective_id=0, has_side_effects=True, vmem_limit_bytes=48 * 1024 * 1024
        ),
    )(*[
        pltpu.with_memory_space_constraint(a, pltpu.HBM)
        for a in (
            page_owner.reshape(1, -1), page_slot.reshape(1, -1),
            key_bias.reshape(1, -1), value_bias.reshape(1, -1),
            request_tokens, request_context,
            hidden, key_weight, value_weight, key_cache, value_cache,
        )
    ])
    keys, values, key_scales, new_value_scales = pl.pallas_call(
        functools.partial(hand_on, heads, hd),
        out_shape=(
            jax.ShapeDtypeStruct(key_cache.shape, b16),
            jax.ShapeDtypeStruct(value_cache.shape, b16),
            jax.ShapeDtypeStruct((heads, slots), b16),
            jax.ShapeDtypeStruct((heads, slots), b16),
        ),
        in_specs=[vm] * 7,
        out_specs=(hbm,) * 4,
        scratch_shapes=[
            pltpu.VMEM((slots, page, hd), b16),
            pltpu.VMEM((heads, slots), b16),
            pltpu.VMEM((heads, slots), b16),
            pltpu.SemaphoreType.DMA((5,)),
        ],
        compiler_params=pltpu.CompilerParams(vmem_limit_bytes=8 * 1024 * 1024),
    )(*held, stored_key_scales.T, value_scales.T)
    return keys, values, key_scales.T, new_value_scales.T


def solution(mesh):
    placed = (
        P("seq", "head"),
        P("head", None),
        P("head", None),
        P("head"),
        P("head"),
        P(),
        P(),
        P(),
        P(),
        P("seq", None, "head"),
        P("seq", None, "head"),
        P("seq", "head"),
        P("seq", "head"),
    )
    return jax.shard_map(
        shards,
        mesh=mesh,
        in_specs=placed,
        out_specs=(
            P("seq", None, "head"),
            P("seq", None, "head"),
            P("seq", "head"),
            P("seq", "head"),
        ),
        check_vma=False,
    )
```

time: 44.2 us -> 40.3 us (0.912); the launches traced: 44.1 us -> 39.5 us
  Pallas kernels: 43.4 us -> 38.8 us
    pallas_call x1, Pallas kernels: 42.3 us -> 37.3 us  [shards(): pl.pallas_call(functools.partial(body, n, cap, heads, hd, page, slots), o...]
where the time goes in v2:
time: 40.3 us; the launch traced here: 39.5 us
  Pallas kernels  38.8 us (96%)
  between operations  0.68 us (2%)
    pallas_call x1, Pallas kernels, shards(): pl.pallas_call(functools.partial(body, n, cap, heads, hd, page, slots), o...  37.3 us
    pallas_call x1, Pallas kernels, shards(): pl.pallas_call(functools.partial(hand_on, heads, hd), out_shape=(jax.Shap...  1.53 us

profile of v2, /device:TPU:0, one launch (start us, length us, event | category | flops | bytes accessed | tf_op | source)
XLA Modules:
  0.0 39.5 jit_solution(10221778552517804612)
XLA Ops:
  0.6 0.0 copy-start
  0.6 0.0 copy-start.1
  0.7 37.3 %shard_map.156 = (bf16[2,79,8,512]{3,2,1,0:T(8,128)(2,1)S(1)}, bf16[80,8,128]{2,1,0:T(8,128)(2,1)S(1)}, bf16[640,640]{1,0:T(8,128)(2,1)S(1)}, f32[640,1]{1,0:T(8,128)S(1)}, f32[80,1,128]{2,1,0:T(1,128)S(1)}) custom-call(s32[1,1024]{1,0:T(1,128)} %bitcast.10, s32[1,1024]{1,0:T(1,128)} %bitcast.11, f32[1,512]{1,0:T(1,128)} %bitcast.12, f32[1,512]{1,0:T(1,128)} %bitcast.13, ...), custom_call_target="tpu_custom_call" | custom-call | tf_op jit(solution)/shard_map/pallas_call | solution.py:389
  38.0 0.0 copy-done
  38.0 0.0 copy-done.1
  38.0 1.5 %shard_map.157 = (bf16[79,8,512]{2,1,0:T(8,128)(2,1)}, bf16[79,8,512]{2,1,0:T(8,128)(2,1)}, bf16[4,79]{1,0:T(4,128)(2,1)}, bf16[4,79]{1,0:T(4,128)(2,1)}) custom-call(bf16[2,79,8,512]{3,2,1,0:T(8,128)(2,1)S(1)} %get-tuple-element.13.held_v, bf16[80,8,128]{2,1,0:T(8,128)(2,1)S(1)} %get-tuple-element.14.last_v, bf16[640,640]{1,0:T(8,128)(2,1)S(1)} %get-tuple-element.15.u_v, ...), custom_call_target="tpu_custom_call" | custom-call | tf_op jit(solution)/shard_map/pallas_call | solution.py:440
Async XLA Ops:
  0.6 37.3 %copy-start = (bf16[79,4]{0,1:T(4,128)(2,1)S(1)}, bf16[79,4]{0,1:T(4,128)(2,1)}, u32[]{:S(2)}) copy-start(bf16[79,4]{0,1:T(4,128)(2,1)} %param.24) | copy-start | bytes 1900
  0.6 37.3 %copy-start.1 = (bf16[79,4]{0,1:T(4,128)(2,1)S(1)}, bf16[79,4]{0,1:T(4,128)(2,1)}, u32[]{:S(2)}) copy-start(bf16[79,4]{0,1:T(4,128)(2,1)} %param.25) | copy-start | bytes 1900

commit v3 on v2

--- a/solution.py
+++ b/solution.py
@@ -20,14 +20,19 @@
     return tuple(zip(edges, edges[1:]))
 
 
-def coded(c, x, scales):
+def coded(u_v, x, slots):
     count, page, hd = x.shape
-    lane = lax.broadcasted_iota(jnp.int32, (1, 1, hd), 2)
-    x = x.astype(jnp.float32)
-    largest = jnp.max(jnp.max(jnp.abs(x), axis=1, keepdims=True), axis=2, keepdims=True)
+    rows = x.astype(jnp.float32).reshape(count * page, hd).astype(jnp.bfloat16)
+    placed = jnp.dot(u_v[...], rows, preferred_element_type=jnp.float32)
+    placed = placed[: slots * page].reshape(slots, page, hd)
+    largest = jnp.max(jnp.max(jnp.abs(placed), axis=1, keepdims=True), axis=2, keepdims=True)
     scale = (largest + eps).astype(jnp.bfloat16).astype(jnp.float32)
-    codes = (x / scale).reshape(count * page, hd)
-    return codes, scales + jnp.where(lane == c, scale, 0.0)
+    return placed / scale, scale
+
+
+def taken(sr_v, slots, page):
+    row = sr_v[...][: slots * page].reshape(slots, page, 1)
+    return jnp.max(row, axis=1, keepdims=True) >= 0.0
 
 
 def body(
@@ -125,7 +130,7 @@
         part = pl.ds(low, high - low)
 
         def send(i, carry):
-            there, spot = i // 4, (me + i) % 4
+            there, spot = jnp.where(me < 8, 3 - i // 4, i // 4), (me + i) % 4
             dest = there * 4 + spot
             k = lax.rem(dest - me + n, n)
             steps = spot % 2 + spot // 2 + there % 2
@@ -155,9 +160,11 @@
             return
         launch(g, lambda steps: steps <= 1)
         if g == len(groups) - 1:
-            for e in range(late, g):
-                launch(e, lambda steps: steps > 1)
-            launch(g, lambda steps: steps > 1)
+            launch(late, lambda steps: steps > 1)
+            for e in range(late + 1, g + 1):
+                launch(e, lambda steps: steps == 2)
+            for e in range(late + 1, g + 1):
+                launch(e, lambda steps: steps == 3)
 
     def post(c):
         swap(c).wait()
@@ -284,7 +291,8 @@
     post(chunks - 1)
 
     unpack_table()
-    written = (sr_v[...] >= 0.0)[: slots * page]
+    written = taken(sr_v, slots, page)
+    head_lane = lax.broadcasted_iota(jnp.int32, (1, 1, hd), 2)
     for i in range(2):
         pltpu.make_async_copy(cache_v.at[i], cache_v.at[i], c_sem.at[i]).wait()
 
@@ -297,12 +305,11 @@
 
         @pl.when(c < chunks - 1)
         def _():
-            codes, scale_v[...] = coded(c, recv_v[c], scale_v[...])
-            placed = jnp.dot(u_v[...], codes.astype(b16), preferred_element_type=f32)
+            codes, scale = coded(u_v, recv_v[c], slots)
+            scale_v[...] += jnp.where(written & (head_lane == c), scale, 0.0)
             lanes = pl.ds(pl.multiple_of((c % heads) * hd, hd), hd)
-            old = cache_v[c // heads, :, :, lanes].astype(f32).reshape(slots * page, hd)
-            new = jnp.where(written, placed[: slots * page], old)
-            cache_v[c // heads, :, :, lanes] = new.reshape(slots, page, hd).astype(b16)
+            old = cache_v[c // heads, :, :, lanes].astype(f32)
+            cache_v[c // heads, :, :, lanes] = jnp.where(written, codes, old).astype(b16)
 
         return carry
 
@@ -334,17 +341,14 @@
     ]
     for copy in copies[:2]:
         copy.start()
-    count = last_v.shape[0]
-    codes, scales = coded(2 * heads - 1, last_v[...], held_scale[...])
-    flat = jnp.broadcast_to(scales, (count, page, hd)).reshape(count * page, hd)
-    both = jnp.concatenate([codes, flat], axis=1).astype(b16)
-    placed = jnp.dot(u_v[...], both, preferred_element_type=f32)[: slots * page]
-    written = (sr_v[...] >= 0.0)[: slots * page]
-    old = held_v[1, :, :, cut:].astype(f32).reshape(slots * page, hd)
-    new = jnp.where(written, placed[:, :hd], old)
-    tail_v[...] = new.reshape(slots, page, hd).astype(b16)
+    written = taken(sr_v, slots, page)
+    head_lane = lax.broadcasted_iota(jnp.int32, (1, 1, hd), 2)
+    codes, scale = coded(u_v, last_v[...], slots)
+    old = held_v[1, :, :, cut:].astype(f32)
+    tail_v[...] = jnp.where(written, codes, old).astype(b16)
     copies[2].start()
-    spread = placed[:, hd:].reshape(slots, page, hd)[:, 0, :]
+    scales = held_scale[...] + jnp.where(written & (head_lane == 2 * heads - 1), scale, 0.0)
+    spread = scales[:, 0, :]
     spread = jnp.concatenate([spread, jnp.zeros((128 - slots % 128, hd), f32)], axis=0)
     spread = jnp.transpose(spread)[:, :slots]
     vs_v[...] = jnp.where(spread[:heads] > 0.0, spread[:heads], ovs_ref[...].astype(f32)).astype(b16)
@@ -393,7 +397,7 @@
             pltpu.VMEM((n * cap, page, hd), b16),
             pltpu.VMEM((srows, rows), b16),
             pltpu.VMEM((srows, 1), f32),
-            pltpu.VMEM((n * cap, 1, hd), f32),
+            pltpu.VMEM((slots, 1, hd), f32),
         ),
         in_specs=[hbm] * 11,
         out_specs=(vm,) * 5,

time: 40.3 us -> 40.1 us (level)
  no operation moved by 1% of the time
where the time goes in v3:
time: 40.1 us; the launch traced here: 39.4 us
  Pallas kernels  38.7 us (97%)
  between operations  0.68 us (2%)
    pallas_call x1, Pallas kernels, shards(): pl.pallas_call(functools.partial(body, n, cap, heads, hd, page, slots), o...  37.3 us
    pallas_call x1, Pallas kernels, shards(): pl.pallas_call(functools.partial(hand_on, heads, hd), out_shape=(jax.Shap...  1.36 us

profile of v3, /device:TPU:0, one launch (start us, length us, event | category | flops | bytes accessed | tf_op | source)
XLA Modules:
  0.0 39.4 jit_solution(4728543707830552022)
XLA Ops:
  0.6 0.0 copy-start
  0.6 0.0 copy-start.1
  0.7 37.3 %shard_map.156 = (bf16[2,79,8,512]{3,2,1,0:T(8,128)(2,1)S(1)}, bf16[80,8,128]{2,1,0:T(8,128)(2,1)S(1)}, bf16[640,640]{1,0:T(8,128)(2,1)S(1)}, f32[640,1]{1,0:T(8,128)S(1)}, f32[79,1,128]{2,1,0:T(1,128)S(1)}) custom-call(s32[1,1024]{1,0:T(1,128)} %bitcast.10, s32[1,1024]{1,0:T(1,128)} %bitcast.11, f32[1,512]{1,0:T(1,128)} %bitcast.12, f32[1,512]{1,0:T(1,128)} %bitcast.13, ...), custom_call_target="tpu_custom_call" | custom-call | tf_op jit(solution)/shard_map/pallas_call | solution.py:393
  38.0 0.0 copy-done
  38.0 0.0 copy-done.1
  38.0 1.4 %shard_map.157 = (bf16[79,8,512]{2,1,0:T(8,128)(2,1)}, bf16[79,8,512]{2,1,0:T(8,128)(2,1)}, bf16[4,79]{1,0:T(4,128)(2,1)}, bf16[4,79]{1,0:T(4,128)(2,1)}) custom-call(bf16[2,79,8,512]{3,2,1,0:T(8,128)(2,1)S(1)} %get-tuple-element.13.held_v, bf16[80,8,128]{2,1,0:T(8,128)(2,1)S(1)} %get-tuple-element.14.last_v, bf16[640,640]{1,0:T(8,128)(2,1)S(1)} %get-tuple-element.15.u_v, ...), custom_call_target="tpu_custom_call" | custom-call | tf_op jit(solution)/shard_map/pallas_call | solution.py:444
Async XLA Ops:
  0.6 37.3 %copy-start = (bf16[79,4]{0,1:T(4,128)(2,1)S(1)}, bf16[79,4]{0,1:T(4,128)(2,1)}, u32[]{:S(2)}) copy-start(bf16[79,4]{0,1:T(4,128)(2,1)} %param.24) | copy-start | bytes 1900
  0.6 37.3 %copy-start.1 = (bf16[79,4]{0,1:T(4,128)(2,1)S(1)}, bf16[79,4]{0,1:T(4,128)(2,1)}, u32[]{:S(2)}) copy-start(bf16[79,4]{0,1:T(4,128)(2,1)} %param.25) | copy-start | bytes 1900
